TPU v7x, 32 devices: a whole 2x2x4 slice. The times are simulated.
32 devices in a mesh: row: 4 (over z), col: 4 (over y, x), layer: 2 (over core).
Axes of the slice: x: 2, y: 2, z: 4, core: 2. Of those that a mesh axis runs over, the one named last changes fastest.
Arguments:
- expression: bfloat16 [6144, 1024], P(('row', 'col'), 'layer'), may hold values from -240 to 240
Outputs:
- connectivity: float32 [6144], P(('row', 'col', 'layer'))
All inputs are finite; a program needn't handle non-finite values.
Results may differ from a plain program's by a relative error of at most 0.00048.
Values may be sent and summed in bfloat16 or wider, within the bound.
A program may use at most 64 MiB of HBM per device.

v0:
```python
import jax
import jax.numpy as jnp
from jax import lax
from jax.sharding import PartitionSpec as P

S = 1024
epsilon = 1e-05


def adjacency(correlation):
    shifted = (1.0 + correlation) * 0.5
    square = shifted * shifted
    fourth = square * square
    eighth = fourth * fourth
    return eighth * fourth


def standardize(values, total, squares):
    average = total / S
    variance = squares / S - average * average
    return ((values - average[:, None]) * lax.rsqrt(variance + epsilon)[:, None]).astype(
        jnp.bfloat16
    )


def pair_products(left, right):
    return lax.dot_general(
        left, right, (((1,), (1,)), ((), ())), preferred_element_type=jnp.float32
    )


def on_device(expression):
    whole = lax.all_gather(expression, "layer", axis=1, tiled=True)
    values = whole.astype(jnp.float32)
    scaled = standardize(values, jnp.sum(values, axis=1), jnp.sum(values * values, axis=1))
    row_genes = lax.all_gather(scaled, "col", axis=0, tiled=True)
    share = scaled.shape[0] // lax.axis_size("layer")
    own_half = lax.dynamic_slice_in_dim(scaled, lax.axis_index("layer") * share, share, 0)
    partial_value = jnp.sum(
        adjacency(
            pair_products(lax.all_gather(own_half, "row", axis=0, tiled=True), row_genes) / S
        ),
        axis=0,
    )
    summed = lax.psum_scatter(partial_value, ("col", "layer"), scatter_dimension=0, tiled=True)
    return summed - 1.0


def solution(mesh):
    placed = (P(("row", "col"), "layer"),)
    return jax.shard_map(
        on_device, mesh=mesh, in_specs=placed, out_specs=P(("row", "col", "layer")), check_vma=False
    )
```

profile of v0, /device:TPU:0, one launch (start us, length us, event | category | flops | bytes accessed | tf_op | source)
XLA Modules:
  0.0 121.1 jit_solution(8612865280336026909)
XLA Ops:
  6.5 0.0 copy-start.1
  6.5 0.0 all-gather.3.cloned.1.call-start
  6.5 2.8 %all_gather.9 = bf16[384,1024]{1,0:T(8,128)(2,1)S(1)} all-gather(bf16[384,512]{1,0:T(8,128)(2,1)} %param.1), channel_id=1, replica_groups=mesh['row'=4,'col'=4,'layer'=2] {'layer'}, dimensions={1}, use_global_device_ids=true | all-gather | bytes 1179648 | tf_op jit(solution)/shard_map/all_gather | solution.py:33
  9.4 0.3 convert_reduce_fusion
  9.7 0.3 fusion.2
  9.9 0.0 copy-start
  10.0 0.9 constant_dynamic-slice_fusion
  10.8 0.0 all-gather.3.cloned.1.call-update
  10.8 0.0 all-gather.5.cloned.1.call-start
  10.9 0.1 copy-done
  11.0 0.6 all-gather.5.cloned.1.call-update
  11.6 0.0 copy-done.1
  11.6 0.6 dynamic-slice
  12.8 37.8 %all-gather.3.cloned.1.call-done = bf16[768,1024]{1,0:T(8,128)(2,1)} async-done(((bf16[192,1024]{1,0:T(8,128)(2,1)}), bf16[768,1024]{1,0:T(8,128)(2,1)}) %all-gather.3.cloned.1.call-update) | async-done | bytes 1572880 | tf_op jit(solution)/shard_map/all_gather | solution.py:41
  50.6 44.6 %all-gather.5.cloned.1.call-done = bf16[1536,1024]{1,0:T(8,128)(2,1)} async-done(((bf16[384,1024]{1,0:T(8,128)(2,1)}), bf16[1536,1024]{1,0:T(8,128)(2,1)}) %all-gather.5.cloned.1.call-update) | async-done | bytes 3145744 | tf_op jit(solution)/shard_map/all_gather | solution.py:36
  95.2 5.6 %fusion = f32[1536]{0:T(1024)S(1)} fusion(bf16[768,1024]{1,0:T(8,128)(2,1)} %all-gather.3.cloned.1.call-done, bf16[1536,1024]{1,0:T(8,128)(2,1)} %all-gather.5.cloned.1.call-done), kind=kOutput, calls=%fused_computation.1 | convolution fusion | flops 2425354752 | bytes 4724736 | tf_op jit(solution)/shard_map/dot_general | solution.py:27
  100.8 12.8 %all-reduce = f32[1536]{0:T(1024)S(1)} all-reduce(f32[1536]{0:T(1024)S(1)} %fusion), channel_id=2, replica_groups=mesh['row'=4,'col'=4,'layer'=2] {'col','layer'}, use_global_device_ids=true, to_apply=%region_3.0.clone | all-reduce | flops 1536 | bytes 12288
  113.6 0.6 dynamic-slice_add_fusion
  (1 shorter events, 0.0 us)
Async XLA Ops:
  6.5 5.1 %copy-start.1 = (u32[32]{0:T(128)S(1)}, u32[32]{0:T(128)}, u32[]{:S(2)}) copy-start(u32[32]{0:T(128)} %constant.29) | copy-start | bytes 388
  6.5 44.1 %all-gather.3.cloned.1.call-start = ((), (), s32[]{:S(2)}) async-start(), calls=%async_computation | async-start | bytes 1966080 | tf_op jit(solution)/shard_map/all_gather | solution.py:41
  9.9 1.1 copy-start
  10.8 84.4 %all-gather.5.cloned.1.call-start = ((), (), s32[]{:S(2)}) async-start(), calls=%async_computation.1 | async-start | bytes 3932160 | tf_op jit(solution)/shard_map/all_gather | solution.py:36
Sparse Core Ops, SparseCore 0:
  11.0 39.6 all-gather.2
  52.5 42.6 all-gather.4
where the time goes:
time: 121 us
  waiting for transfers between devices  83 us (69%)
  blocking collectives  15.6 us (13%)
  between operations  14.1 us (12%)
  matrix products  5.59 us (5%)
  local copies, waits for them, and re-layouts  1.56 us (1%)
  other arithmetic  1.22 us (1%)
    all_gather x1, waiting for transfers between devices, on_device(): row_genes = lax.all_gather(scaled, 'col', axis=0, tiled=True)  44.6 us
    all_gather x1, waiting for transfers between devices, on_device(): lax.all_gather(own_half, 'row', axis=0, tiled=True)  37.8 us
    unnamed x1, blocking collectives  12.8 us
    dot_general x1, matrix products, pair_products(): lax.dot_general(left, right, (((1,), (1,)), ((), ())), preferred_element_...  5.59 us
    all_gather x1, blocking collectives, on_device(): whole = lax.all_gather(expression, 'layer', axis=1, tiled=True)  2.82 us
  transfers between devices with their start and end apart: 2, of which 2 were waited for; matrix products, arithmetic and copies ran while one was open for 0% of the time, Pallas kernels for 0%

commit v1 on v0

--- a/solution.py
+++ b/solution.py
@@ -33,7 +33,12 @@
     whole = lax.all_gather(expression, "layer", axis=1, tiled=True)
     values = whole.astype(jnp.float32)
     scaled = standardize(values, jnp.sum(values, axis=1), jnp.sum(values * values, axis=1))
-    row_genes = lax.all_gather(scaled, "col", axis=0, tiled=True)
+    ring = [scaled]
+    for hop in range(3):
+        ring.append(lax.ppermute(ring[-1], "col", [(dev, (dev + 1) % 4) for dev in range(4)]))
+    row_genes = jnp.roll(
+        jnp.concatenate(ring[::-1], axis=0), (lax.axis_index("col") + 1) * ring[0].shape[0], axis=0
+    )
     share = scaled.shape[0] // lax.axis_size("layer")
     own_half = lax.dynamic_slice_in_dim(scaled, lax.axis_index("layer") * share, share, 0)
     partial_value = jnp.sum(

time: 121 us -> 104 us (0.86)
  waiting for transfers between devices: 83 us -> 55.1 us
  local copies, waits for them, and re-layouts: 1.56 us -> 6.99 us
  starting transfers between devices: 0.04 us -> 3.69 us
  other arithmetic: 1.22 us -> 3.55 us
    ppermute x0 -> x3, waiting for transfers between devices: none -> 55 us  [on_device(): lax.ppermute(ring[-1], 'col', [(dev, (dev + 1) % 4) for dev in range(4)])]
    all_gather x1 -> x0, waiting for transfers between devices: 44.6 us -> none  [on_device(): row_genes = lax.all_gather(scaled, 'col', axis=0, tiled=True)]
    all_gather x1, waiting for transfers between devices: 37.8 us -> 0.01 us  [on_device(): lax.all_gather(own_half, 'row', axis=0, tiled=True)]
    unnamed x5 -> x9, local copies, waits for them, and re-layouts: 0.7 us -> 6.22 us
    ppermute x0 -> x3, starting transfers between devices: none -> 3.69 us  [on_device(): lax.ppermute(ring[-1], 'col', [(dev, (dev + 1) % 4) for dev in range(4)])]
  transfers between devices with their start and end apart: 2 -> 4, of which waited for: 2 -> 3; matrix products, arithmetic and copies ran while one was open for 0% -> 9% of each run, Pallas kernels for 0% -> 0%
where the time goes in v1:
time: 104 us
  waiting for transfers between devices  55.1 us (53%)
  blocking collectives  14.9 us (14%)
  between operations  14.1 us (14%)
  local copies, waits for them, and re-layouts  6.99 us (7%)
  matrix products  5.74 us (6%)
  starting transfers between devices  3.69 us (4%)
  other arithmetic  3.55 us (3%)
    ppermute x3, waiting for transfers between devices, on_device(): lax.ppermute(ring[-1], 'col', [(dev, (dev + 1) % 4) for dev in range(4)])  55 us
    unnamed x1, blocking collectives  12 us
    unnamed x9, local copies, waits for them, and re-layouts  6.22 us
    dot_general x1, matrix products, pair_products(): lax.dot_general(left, right, (((1,), (1,)), ((), ())), preferred_element_...  5.74 us
    ppermute x3, starting transfers between devices, on_device(): lax.ppermute(ring[-1], 'col', [(dev, (dev + 1) % 4) for dev in range(4)])  3.69 us
    all_gather x1, blocking collectives, on_device(): whole = lax.all_gather(expression, 'layer', axis=1, tiled=True)  2.82 us
  transfers between devices with their start and end apart: 4, of which 3 were waited for; matrix products, arithmetic and copies ran while one was open for 9% of the time, Pallas kernels for 0%

profile of v1, /device:TPU:0, one launch (start us, length us, event | category | flops | bytes accessed | tf_op | source)
XLA Modules:
  0.0 104.0 jit_solution(6751957552784910214)
XLA Ops:
  6.5 0.0 all-gather.2.cloned.1.call-start
  6.5 2.8 %all_gather.6 = bf16[384,1024]{1,0:T(8,128)(2,1)S(1)} all-gather(bf16[384,512]{1,0:T(8,128)(2,1)} %param.1), channel_id=1, replica_groups=mesh['row'=4,'col'=4,'layer'=2] {'layer'}, dimensions={1}, use_global_device_ids=true | all-gather | bytes 1179648 | tf_op jit(solution)/shard_map/all_gather | solution.py:33
  9.4 0.3 convert_reduce_fusion
  9.7 0.3 fusion.3
  9.9 2.9 %collective-permute-start = (bf16[384,1024]{1,0:T(8,128)(2,1)S(1)}, bf16[384,1024]{1,0:T(8,128)(2,1)S(1)}, u32[]{:S(2)}, u32[]{:S(2)}) collective-permute-start(bf16[384,1024]{1,0:T(8,128)(2,1)S(1)} %fusion.3), channel_id=1, source_target_pairs={{0,2},{2,4},{4,6},{6,0},{1,3},{3,5},{5,7},{7,1},{8,10},{10,12},{12... | collective-permute-start | bytes 2359304 | tf_op jit(solution)/shard_map/ppermute | solution.py:38
  12.8 18.8 %collective-permute-done = bf16[384,1024]{1,0:T(8,128)(2,1)S(1)} collective-permute-done((bf16[384,1024]{1,0:T(8,128)(2,1)S(1)}, bf16[384,1024]{1,0:T(8,128)(2,1)S(1)}, u32[]{:S(2)}, u32[]{:S(2)}) %collective-permute-start) | collective-permute-done | bytes 786464 | tf_op jit(solution)/shard_map/ppermute | solution.py:38
  31.6 0.8 collective-permute-start.1
  32.4 0.8 constant_dynamic-slice_fusion
  33.2 0.0 all-gather.2.cloned.1.call-update
  33.2 18.3 %collective-permute-done.1 = bf16[384,1024]{1,0:T(8,128)(2,1)S(1)} collective-permute-done((bf16[384,1024]{1,0:T(8,128)(2,1)S(1)}, bf16[384,1024]{1,0:T(8,128)(2,1)S(1)}, u32[]{:S(2)}, u32[]{:S(2)}) %collective-permute-start.1) | collective-permute-done | bytes 786464 | tf_op jit(solution)/shard_map/ppermute | solution.py:38
  51.6 0.0 collective-permute-start.2
  51.6 0.6 dynamic-slice
  52.8 17.9 %collective-permute-done.2 = bf16[384,1024]{1,0:T(8,128)(2,1)S(1)} collective-permute-done((bf16[384,1024]{1,0:T(8,128)(2,1)S(1)}, bf16[384,1024]{1,0:T(8,128)(2,1)S(1)}, u32[]{:S(2)}, u32[]{:S(2)}) %collective-permute-start.2) | collective-permute-done | bytes 786464 | tf_op jit(solution)/shard_map/ppermute | solution.py:38
  70.7 0.9 constant_dynamic-update-slice_fusion.7
  71.6 1.0 constant_dynamic-update-slice_fusion.6
  72.6 0.9 constant_dynamic-update-slice_fusion.5
  73.5 1.1 %constant_dynamic-update-slice_fusion.4 = bf16[3072,1024]{1,0:T(8,128)(2,1)} fusion(bf16[3072,1024]{1,0:T(8,128)(2,1)} %constant_dynamic-update-slice_fusion.5, f32[384]{0:T(512)S(1)} %get-tuple-element.8, f32[384]{0:T(512)S(1)} %get-tuple-element.7, bf16[384,1024]{1,0:T(8,128)(2,1)S(1)} %all_gather.6), kind=kLoop, calls=%fused_computation.13 | loop fusion | flops 1572864 | bytes 1575936
  74.7 0.9 constant_dynamic-update-slice_fusion.3
  75.6 0.9 constant_dynamic-update-slice_fusion.2
  76.5 0.9 constant_dynamic-update-slice_fusion.1
  77.5 1.2 %constant_dynamic-update-slice_fusion = bf16[3072,1024]{1,0:T(8,128)(2,1)} fusion(bf16[3072,1024]{1,0:T(8,128)(2,1)} %constant_dynamic-update-slice_fusion.1, f32[384]{0:T(512)S(1)} %get-tuple-element.8, f32[384]{0:T(512)S(1)} %get-tuple-element.7, bf16[384,1024]{1,0:T(8,128)(2,1)S(1)} %all_gather.6), kind=kLoop, calls=%fused_computation.9 | loop fusion | flops 1572864 | bytes 1575936 | tf_op jit(solution)/shard_map/jit(_roll_dynamic)/concatenate | solution.py:39
  78.7 5.7 %fusion = f32[1536]{0:T(1024)S(1)} fusion(bf16[768,1024]{1,0:T(8,128)(2,1)} %all-gather.2.cloned.1.call-done, bf16[3072,1024]{1,0:T(8,128)(2,1)} %constant_dynamic-update-slice_fusion, s32[]{:T(128)S(6)} %select_n.18), kind=kOutput, calls=%fused_computation.1 | convolution fusion | flops 2425354752 | bytes 4724740 | tf_op jit(solution)/shard_map/dot_general | solution.py:27
  84.4 12.0 %all-reduce = f32[1536]{0:T(1024)S(1)} all-reduce(f32[1536]{0:T(1024)S(1)} %fusion), channel_id=2, replica_groups=mesh['row'=4,'col'=4,'layer'=2] {'col','layer'}, use_global_device_ids=true, to_apply=%region_3.4.clone | all-reduce | flops 1536 | bytes 12288
  96.5 0.6 dynamic-slice_add_fusion
  (4 shorter events, 0.0 us)
Async XLA Ops:
  6.5 45.0 %copy-start = (u32[32]{0:T(128)S(1)}, u32[32]{0:T(128)}, u32[]{:S(2)}) copy-start(u32[32]{0:T(128)} %constant.53) | copy-start | bytes 388
  6.5 72.1 %all-gather.2.cloned.1.call-start = ((), (), s32[]{:S(2)}) async-start(), calls=%async_computation | async-start | bytes 1966080 | tf_op jit(solution)/shard_map/all_gather | solution.py:46
  9.9 21.7 %collective-permute-start = (bf16[384,1024]{1,0:T(8,128)(2,1)S(1)}, bf16[384,1024]{1,0:T(8,128)(2,1)S(1)}, u32[]{:S(2)}, u32[]{:S(2)}) collective-permute-start(bf16[384,1024]{1,0:T(8,128)(2,1)S(1)} %fusion.3), channel_id=1, source_target_pairs={{0,2},{2,4},{4,6},{6,0},{1,3},{3,5},{5,7},{7,1},{8,10},{10,12},{12... | collective-permute-start | bytes 2359304 | tf_op jit(solution)/shard_map/ppermute | solution.py:38
  31.6 19.9 %collective-permute-start.1 = (bf16[384,1024]{1,0:T(8,128)(2,1)S(1)}, bf16[384,1024]{1,0:T(8,128)(2,1)S(1)}, u32[]{:S(2)}, u32[]{:S(2)}) collective-permute-start(bf16[384,1024]{1,0:T(8,128)(2,1)S(1)} %collective-permute-done), channel_id=1, source_target_pairs={{0,2},{2,4},{4,6},{6,0},{1,3},{3,5},{5,7},{7,1},{8,10},{10,12},{12... | collective-permute-start | bytes 2359304 | tf_op jit(solution)/shard_map/ppermute | solution.py:38
  51.6 19.2 %collective-permute-start.2 = (bf16[384,1024]{1,0:T(8,128)(2,1)S(1)}, bf16[384,1024]{1,0:T(8,128)(2,1)S(1)}, u32[]{:S(2)}, u32[]{:S(2)}) collective-permute-start(bf16[384,1024]{1,0:T(8,128)(2,1)S(1)} %collective-permute-done.1), channel_id=1, source_target_pairs={{0,2},{2,4},{4,6},{6,0},{1,3},{3,5},{5,7},{7,1},{8,10},{10,12},{12... | collective-permute-start | bytes 2359304 | tf_op jit(solution)/shard_map/ppermute | solution.py:38
Sparse Core Ops, SparseCore 0:
  33.3 38.2 all-gather.1
